TPU v7x, 32 devices: a whole 2x2x4 slice. The times are simulated.
32 devices in a mesh: tm: 8 (over z, y), space: 4 (over x, core).
Axes of the slice: x: 2, y: 2, z: 4, core: 2. Of those that a mesh axis runs over, the one named last changes fastest.
Arguments:
- density: bfloat16 [2048, 128, 128], P('tm', 'space'), may hold values from -6 to 6
- active: int32 [2048], P('tm'), may hold values from 1 to 128
- neighbours: int32 [128, 8], P('space'), may hold values from 0 to 127, as said below
- near_blocks: bfloat16 [2, 128, 8, 128, 128], P(None, 'space'), may hold values from -0.125 to 0.125
- to_moments: bfloat16 [64, 128, 128], P(None, 'space'), may hold values from -0.046875 to 0.046875
- from_moments: bfloat16 [64, 128, 128], P(None, 'space'), may hold values from -0.75 to 0.75
- decay_rates: float32 [64], replicated, may hold values from 9.765625e-05 to 0.05, as said below
- lengths: float32 [2048], P('tm'), may hold values from 0.5 to 1024, as said below
Outputs:
- potential: bfloat16 [2048, 128, 128], P('tm', 'space')
Inputs may be any that keep to these rules, and one draw needn't show every extreme that they name: `neighbours`: every entry of row c lies within 8 of c; each row names c - 8 and c + 8, clipped to the clusters that exist. `decay_rates`: positive rates. Positive lengths.
All inputs are finite; a program needn't handle non-finite values.
Results may differ from a plain program's by a relative error of at most 0.0085.
Values may be sent and summed in bfloat16 or wider, within the bound.
A program may use at most 128 MiB of HBM per device.

v0:
```python
import functools
import math

import jax
import jax.numpy as jnp
from jax import lax
from jax.experimental import pallas as pl
from jax.experimental.pallas import tpu as pltpu
from jax.sharding import PartitionSpec as P

REACH = 8
PAD = 16
VMEM = 67043328
MESH = pl.DeviceIdType.MESH
F32, BF16 = jnp.float32, jnp.bfloat16


def spread(row):
    return jnp.broadcast_to(row, (128, row.shape[1])).T


def kernel(n_tm, n_space, dens, active, nbrs, blocks, to_m, from_m, rates, lengths,
           near, from_v, act, scaled_o, dens_v, flat, work, halo, halo_prev, row_out, row_in, wb, to_raw, from_raw, to_v,
           part_out, part_in, keep, tot_out, tot_in, state,
           in_sem, w_sem, halo_sem, row_sem, part_ssem, part_rsem, tot_ssem, tot_rsem):
    T, C, E = dens_v.shape
    M = to_raw.shape[0]
    J = wb.shape[2]
    H = T // 2
    tm, sp = lax.axis_index("tm"), lax.axis_index("space")
    first = sp * C

    c_dens = pltpu.make_async_copy(dens, dens_v, in_sem.at[0])
    c_to = pltpu.make_async_copy(to_m, to_raw, in_sem.at[1])
    c_from = pltpu.make_async_copy(from_m, from_raw, in_sem.at[2])
    c_to.start()
    c_dens.start()
    c_from.start()
    barrier = pltpu.get_barrier_semaphore()

    def greet(t, s):
        pl.semaphore_signal(barrier, inc=1, device_id={"tm": t, "space": s}, device_id_type=MESH)

    for d in range(1, n_space):
        greet(tm, lax.rem(sp + d, n_space))
    for d in range(1, n_tm):
        greet(lax.rem(tm + d, n_tm), sp)
    one, nil = jnp.int32(1), jnp.int32(0)
    has = {-1: (tm > 0, sp > 0), 1: (tm < n_tm - 1, sp < n_space - 1)}
    corners = nil
    for dt in (-1, 1):
        for ds in (-1, 1):
            there = jnp.logical_and(has[dt][0], has[ds][1])
            corners = corners + jnp.where(there, one, nil)

            @pl.when(there)
            def _(dt=dt, ds=ds):
                greet(tm + dt, sp + ds)

    def w_copy(c):
        return pltpu.make_async_copy(blocks.at[:, c], wb.at[:, c], w_sem.at[c])

    for h in range(2):
        act[h * H:(h + 1) * H, :] = spread(active[h:h + 1, :].astype(F32))

    TB = 16

    def group(raw, n):
        @pl.loop(0, n // TB)
        def _(i):
            x = raw[pl.ds(i * TB, TB)].astype(F32)
            for q in range(C // 8):
                at = pl.multiple_of(q * n * 8 + i * TB * 8, TB * 8)
                flat[pl.ds(at, TB * 8), :] = x[:, q * 8:q * 8 + 8].reshape(TB * 8, E)

    def cluster(g, n):
        return flat[pl.ds(g // 8 * (n * 8) + g % 8, n, stride=8), :]

    def expand(raw, dst):
        group(raw, M)

        @pl.loop(0, C)
        def _(g):
            x = cluster(g, M).astype(BF16)
            dst[g, 0:M, :] = x
            dst[g, M:2 * M, :] = x

    c_to.wait()
    expand(to_raw, to_v)
    c_dens.wait()
    for lo, hi in ((REACH, C - REACH), (0, REACH), (C - REACH, C)):
        @pl.loop(lo, hi)
        def _(c):
            w_copy(c).start()

    gid = lax.broadcasted_iota(jnp.int32, (C, E), 0).astype(F32) + first.astype(F32)
    row_out[...] = jnp.where(gid < act[T - 1:T, :], dens_v[T - 1].astype(F32), 0.0)
    c_from.wait()
    expand(from_raw, from_v)
    pl.semaphore_wait(barrier, n_space - 1 + n_tm - 1 + corners)

    def row_copy(ds):
        if ds == 0:
            src, dst = row_out, row_in.at[pl.ds(REACH, C)]
        elif ds == 1:
            src, dst = row_out.at[pl.ds(C - REACH, REACH)], row_in.at[pl.ds(0, REACH)]
        else:
            src, dst = row_out.at[pl.ds(0, REACH)], row_in.at[pl.ds(REACH + C, REACH)]
        return pltpu.make_async_remote_copy(
            src_ref=src, dst_ref=dst, send_sem=row_sem.at[0, ds + 1], recv_sem=row_sem.at[1, ds + 1],
            device_id={"tm": tm + 1, "space": sp + ds}, device_id_type=MESH)

    def halo_copy(ds, h):
        k = (1 - ds) // 2
        return pltpu.make_async_remote_copy(
            src_ref=dens_v.at[pl.ds(h * H, H), pl.ds(C - REACH if ds == 1 else 0, REACH), :],
            dst_ref=halo.at[k, pl.ds(h * H, H)],
            send_sem=halo_sem.at[0, k, h], recv_sem=halo_sem.at[1, k, h],
            device_id={"tm": tm, "space": sp + ds}, device_id_type=MESH)

    def halo_send(h):
        for ds in (1, -1):
            @pl.when(on_space(ds))
            def _(ds=ds):
                halo_copy(ds, h).start()

    def on_space(ds):
        return True if ds == 0 else has[ds][1]

    for ds in (0, 1, -1):
        @pl.when(jnp.logical_and(has[1][0], on_space(ds)))
        def _(ds=ds):
            row_copy(ds).start()
    halo_send(0)

    group(dens_v, T)

    @pl.loop(0, C)
    def _(g):
        live = (first + g).astype(F32) < act[...]
        work[REACH + g, 0:T, :] = jnp.where(live, cluster(g, T), 0.0).astype(BF16)

    lane = lax.broadcasted_iota(jnp.int32, (H, 2 * M), 1)
    low = lane < M
    total = jnp.zeros((T, 2 * M), F32)
    GB = 8
    for k in range(C // GB):
        a = jnp.concatenate([work[REACH + k * GB + i, 0:T, :] for i in range(GB)], axis=1)
        b = jnp.concatenate([to_v[k * GB + i] for i in range(GB)], axis=1)
        total = total + lax.dot_general(a, b, (((1,), (1,)), ((), ())), preferred_element_type=F32)
    part = jnp.where(low, total[0:H], total[H:T])
    keep[0] = part
    part_out[...] = part.astype(BF16)

    def part_copy(d):
        return pltpu.make_async_remote_copy(
            src_ref=part_out, dst_ref=part_in.at[sp], send_sem=part_ssem.at[d], recv_sem=part_rsem.at[sp],
            device_id={"tm": tm, "space": lax.rem(sp + d, n_space)}, device_id_type=MESH)

    for d in range(1, n_space):
        part_copy(d).start()
    halo_send(1)

    @pl.when(tm == 0)
    def _():
        row_in[...] = jnp.zeros_like(row_in)

    for ds in (0, 1, -1):
        there = has[-1][0] if ds == 0 else jnp.logical_and(has[-1][0], has[-ds][1])

        @pl.when(there)
        def _(ds=ds):
            row_copy(ds).wait_recv()
    top = lax.broadcasted_iota(jnp.int32, (PAD, E), 0) == 0

    @pl.loop(0, C + 2 * REACH)
    def _(g):
        r = jnp.broadcast_to(row_in[pl.ds(g, 1), :], (PAD, E))
        work[g, T:T + PAD, :] = jnp.where(top, r, 0.0).astype(BF16)

    first_row = lax.broadcasted_iota(jnp.int32, (T, E), 0) == 0

    def near_field(c):
        w_copy(c).wait()
        rows = [jnp.clip(nbrs[j, c] - first + REACH, 0, C + 2 * REACH - 1) for j in range(J)]
        picked = jnp.concatenate([work[i] for i in rows], axis=1)
        w = jnp.concatenate([wb[0, c].reshape(J * E, E), wb[1, c].reshape(J * E, E)], axis=1)
        both = jnp.dot(picked, w, preferred_element_type=F32)
        late = both[:, E:]
        late = jnp.where(first_row, late[T:T + 1, :], pltpu.roll(late[0:T], 1, 0))
        near[c] = both[0:T, 0:E] + late

    pl.loop(REACH, C - REACH)(near_field)

    moment = keep[0]
    for d in range(1, n_space):
        k = lax.rem(sp + n_space - d, n_space)
        pltpu.make_async_remote_copy(
            src_ref=part_out, dst_ref=part_in.at[k], send_sem=part_ssem.at[d], recv_sem=part_rsem.at[k],
            device_id={"tm": tm, "space": k}, device_id_type=MESH).wait_recv()
        moment = moment + part_in[k].astype(F32)
    r = rates[...]
    rr = jnp.concatenate([r, r], axis=1)
    span = jnp.where(low, spread(lengths[0:1, :]), spread(lengths[1:2, :]))
    fall = jnp.exp(-rr * span)
    pos = lax.broadcasted_iota(jnp.int32, (H, 2 * M), 0)
    d = 1
    while d < H:
        start = pos < d
        moment = fall * jnp.where(start, 0.0, pltpu.roll(moment, d, 0)) + moment
        fall = fall * jnp.where(start, 1.0, pltpu.roll(fall, d, 0))
        d *= 2
    keep[0] = jnp.where(pos < 1, 0.0, pltpu.roll(moment, 1, 0))
    keep[1] = jnp.where(pos < 1, 1.0, pltpu.roll(fall, 1, 0))
    end_b = jnp.broadcast_to(moment[H - 1:H, :], (8, 2 * M))
    end_a = jnp.broadcast_to(fall[H - 1:H, :], (8, 2 * M))
    low8 = low[0:8]
    roll_b, roll_a = pltpu.roll(end_b, M, 1), pltpu.roll(end_a, M, 1)
    tot_out[0:8] = end_a * roll_a
    tot_out[8:16] = jnp.where(low8, roll_a * end_b + roll_b, end_a * roll_b + end_b)

    def tot_copy(d):
        return pltpu.make_async_remote_copy(
            src_ref=tot_out, dst_ref=tot_in.at[tm], send_sem=tot_ssem.at[d], recv_sem=tot_rsem.at[tm],
            device_id={"tm": tm + d, "space": sp}, device_id_type=MESH)

    for d in range(1, n_tm):
        @pl.when(tm + d < n_tm)
        def _(d=d):
            tot_copy(d).start()

    near_side = jnp.where(lax.rem(sp, 2) == 1, nil, one)
    for k in (near_side, one - near_side):
        other = sp + 2 * k - 1

        @pl.when(jnp.logical_and(other >= 0, other < n_space))
        def _(k=k, other=other):
            for h in range(2):
                pltpu.make_async_remote_copy(
                    src_ref=dens_v.at[pl.ds(h * H, H), pl.ds(0, REACH), :], dst_ref=halo.at[k, pl.ds(h * H, H)],
                    send_sem=halo_sem.at[0, k, h], recv_sem=halo_sem.at[1, k, h],
                    device_id={"tm": tm, "space": other}, device_id_type=MESH).wait_recv()

            @pl.loop(0, T // 32)
            def _(i):
                x = halo[k, pl.ds(i * 32, 32)].astype(F32)
                flat[pl.ds(pl.multiple_of(i * 32 * REACH, 32 * REACH), 32 * REACH), :] = x.reshape(32 * REACH, E)

            begin = k * (REACH + C)

            @pl.loop(0, REACH)
            def _(g):
                x = flat[pl.ds(g, T, stride=REACH), :]
                live = (first - REACH + begin + g).astype(F32) < act[...]
                work[begin + g, 0:T, :] = jnp.where(live, x, 0.0).astype(BF16)

        @pl.loop(0, REACH)
        def _(i):
            near_field(i + k * (C - REACH))

    state[...] = jnp.zeros_like(state)
    for k in range(n_tm - 1):
        @pl.when(k < tm)
        def _(k=k):
            pltpu.make_async_remote_copy(
                src_ref=tot_out, dst_ref=tot_in.at[k], send_sem=tot_ssem.at[0], recv_sem=tot_rsem.at[k],
                device_id={"tm": jnp.int32(k), "space": sp}, device_id_type=MESH).wait_recv()
            state[...] = tot_in[k, 0:8] * state[...] + tot_in[k, 8:16]
    s = state[...]
    arrive = jnp.where(low8, s, roll_a * s + roll_b)[0:1]
    scaled = (keep[1] * arrive + keep[0]) * jnp.sqrt(2.0 * rr)
    scaled_o[0:H] = jnp.where(low, scaled, 0.0).astype(BF16)
    scaled_o[H:T] = jnp.where(low, 0.0, scaled).astype(BF16)


    for d in range(1, n_space):
        part_copy(d).wait_send()
    for d in range(1, n_tm):
        @pl.when(tm + d < n_tm)
        def _(d=d):
            tot_copy(d).wait_send()
    for ds in (0, 1, -1):
        @pl.when(jnp.logical_and(has[1][0], on_space(ds)))
        def _(ds=ds):
            row_copy(ds).wait_send()
    for ds in (1, -1):
        @pl.when(on_space(ds))
        def _(ds=ds):
            for h in range(2):
                halo_copy(ds, h).wait_send()


def finish(near, from_v, act, scaled_o, out, stage, out_v, out_sem):
    C, T, E = near.shape
    GB = 8
    first = lax.axis_index("space") * C
    scaled = scaled_o[...]

    def out_copy(k):
        return pltpu.make_async_copy(out_v.at[k], out.at[:, pl.ds(k * GB, GB), :], out_sem.at[k])

    for k in range(C // GB):
        for i in range(0, GB, 2):
            g = k * GB + i
            far = jnp.dot(scaled, jnp.concatenate([from_v[g], from_v[g + 1]], axis=1), preferred_element_type=F32)
            for u in range(2):
                live = (first + g + u).astype(F32) < act[...]
                pot = jnp.where(live, near[g + u] + far[:, u * E:(u + 1) * E], 0.0)
                stage[pl.ds(i + u, T, stride=GB), :] = pot
        out_v[k] = stage[...].reshape(T, GB, E).astype(BF16)
        out_copy(k).start()
    for k in range(C // GB):
        out_copy(k).wait()


def solution(mesh):
    n_tm, n_space = mesh.shape["tm"], mesh.shape["space"]

    def local(density, active, neighbours, near_blocks, to_moments, from_moments, decay_rates, lengths):
        T, C, E = density.shape
        J = neighbours.shape[1]
        M = decay_rates.shape[0]
        H, W = T // 2, C + 2 * REACH
        vm = lambda shape, t: pltpu.VMEM(shape, t)
        dma = pltpu.SemaphoreType.DMA
        kept = [((C, T, E), F32), ((C, 2 * M, E), BF16), ((T, 128), F32), ((T, 2 * M), BF16)]
        room = sum(math.prod(s) * jnp.dtype(t).itemsize for s, t in kept) + 32 * 1024
        anyspec = pl.BlockSpec(memory_space=pl.ANY)
        vspec = pl.BlockSpec(memory_space=pltpu.VMEM)
        held = pl.pallas_call(
            functools.partial(kernel, n_tm, n_space),
            out_shape=[pltpu.VMEM(s, t) for s, t in kept],
            in_specs=[anyspec, vspec, pl.BlockSpec(memory_space=pltpu.SMEM), anyspec, anyspec, anyspec, vspec, vspec],
            out_specs=[vspec] * 4,
            scratch_shapes=[
                vm((T, C, E), BF16), vm((T * C, E), F32), vm((W, T + PAD, E), BF16),
                vm((2, T, REACH, E), BF16), vm((8, 128), F32), vm((C, E), F32), vm((W, E), F32),
                vm((2, C, J, E, E), BF16), vm((M, C, E), BF16), vm((M, C, E), BF16),
                vm((C, 2 * M, E), BF16),
                vm((H, 2 * M), BF16), vm((n_space, H, 2 * M), BF16), vm((2, H, 2 * M), F32),
                vm((16, 2 * M), F32), vm((n_tm, 16, 2 * M), F32), vm((8, 2 * M), F32),
                dma((3,)), dma((C,)), dma((2, 2, 2)), dma((2, 3)), dma((n_space,)), dma((n_space,)),
                dma((n_tm,)), dma((n_tm,)),
            ],
            compiler_params=pltpu.CompilerParams(
                collective_id=0, has_side_effects=True, vmem_limit_bytes=VMEM - room),
        )(density, active.reshape(2, H), neighbours.T, near_blocks, to_moments, from_moments,
          decay_rates.reshape(1, M), lengths.reshape(2, H))
        return pl.pallas_call(
            finish,
            out_shape=jax.ShapeDtypeStruct((T, C, E), BF16),
            in_specs=[vspec] * 4,
            out_specs=anyspec,
            scratch_shapes=[vm((T * 8, E), F32), vm((C // 8, T, 8, E), BF16), dma((C // 8,))],
            compiler_params=pltpu.CompilerParams(vmem_limit_bytes=16 * 1024 * 1024),
        )(*held)

    placed = (
        P("tm", "space", None), P("tm"), P("space", None), P(None, "space", None, None, None),
        P(None, "space", None), P(None, "space", None), P(), P("tm"),
    )
    return jax.shard_map(
        local, mesh=mesh, in_specs=placed, out_specs=P("tm", "space", None), check_vma=False)
```

profile of v0, /device:TPU:0, one launch (start us, length us, event | category | flops | bytes accessed | tf_op | source)
XLA Modules:
  0.0 23.5 jit_solution(17550548634797024740)
XLA Ops:
  0.0 21.5 %shard_map.82 = (f32[32,256,128]{2,1,0:T(8,128)S(1)}, bf16[32,128,128]{2,1,0:T(8,128)(2,1)S(1)}, f32[256,128]{1,0:T(8,128)S(1)}, bf16[256,128]{1,0:T(8,128)(2,1)S(1)}) custom-call(bf16[256,32,128]{2,1,0:T(8,128)(2,1)} %dens.1, s32[2,128]{1,0:T(2,128)} %bitcast.5, s32[8,32]{1,0:T(8,128)} %bitcast.4, bf16[2,32,8,128,128]{4,3,2,1,0:T(8,128)(2,1)} %blocks.1, ...), custom_call_target="tpu_custom_call" | custom-call | tf_op jit(solution)/shard_map/pallas_call | solution.py:330
  21.6 1.9 %shard_map.83 = bf16[256,32,128]{2,1,0:T(8,128)(2,1)} custom-call(f32[32,256,128]{2,1,0:T(8,128)S(1)} %get-tuple-element.9.near, bf16[32,128,128]{2,1,0:T(8,128)(2,1)S(1)} %get-tuple-element.10.from_v, f32[256,128]{1,0:T(8,128)S(1)} %get-tuple-element.11.act, bf16[256,128]{1,0:T(8,128)(2,1)S(1)} %get-tuple-element.12.scaled_o), custom_call_target="tpu_custom_call" | custom-call | tf_op jit(solution)/shard_map/pallas_call | solution.py:349
where the time goes:
time: 23.6 us; the launch traced here: 23.5 us
  Pallas kernels  23.5 us (100%)
    pallas_call x1, Pallas kernels, local(): pl.pallas_call(functools.partial(kernel, n_tm, n_space), out_shape=[pltpu...  21.5 us
    pallas_call x1, Pallas kernels, local(): pl.pallas_call(finish, out_shape=jax.ShapeDtypeStruct((T, C, E), BF16), i...  1.95 us

commit v1 on v0

--- a/solution.py
+++ b/solution.py
@@ -9,6 +9,8 @@
 from jax.sharding import PartitionSpec as P
 
 REACH = 8
+U = 8
+DC = 4
 PAD = 16
 VMEM = 67043328
 MESH = pl.DeviceIdType.MESH
@@ -19,10 +21,22 @@
     return jnp.broadcast_to(row, (128, row.shape[1])).T
 
 
-def kernel(n_tm, n_space, dens, active, nbrs, blocks, to_m, from_m, rates, lengths,
-           near, from_v, act, scaled_o, dens_v, flat, work, halo, halo_prev, row_out, row_in, wb, to_raw, from_raw, to_v,
+def swap16():
+    r = lax.broadcasted_iota(jnp.int32, (256, 256), 0)
+    s = lax.broadcasted_iota(jnp.int32, (256, 256), 1)
+    return jnp.where(s == (r % 16) * 16 + r // 16, 1.0, 0.0).astype(BF16)
+
+
+def swap8():
+    r = lax.broadcasted_iota(jnp.int32, (256, 256), 0)
+    s = lax.broadcasted_iota(jnp.int32, (256, 256), 1)
+    return jnp.where(s == (r % 32) * 8 + r // 32, 1.0, 0.0).astype(BF16)
+
+
+def kernel(n_tm, n_space, dens, active_h, nbrs_h, blocks, to_m, from_m, rates_h, lengths_h,
+           near, from_v, act, scaled_o, dens_v, work, active, nbrs, rates, lengths, perm, halo, halo_prev, row_out, row_in, wb, to_raw, from_raw, to_v,
            part_out, part_in, keep, tot_out, tot_in, state,
-           in_sem, w_sem, halo_sem, row_sem, part_ssem, part_rsem, tot_ssem, tot_rsem):
+           in_sem, dens_sem, w_sem, halo_sem, row_sem, part_ssem, part_rsem, tot_ssem, tot_rsem):
     T, C, E = dens_v.shape
     M = to_raw.shape[0]
     J = wb.shape[2]
@@ -30,11 +44,21 @@
     tm, sp = lax.axis_index("tm"), lax.axis_index("space")
     first = sp * C
 
-    c_dens = pltpu.make_async_copy(dens, dens_v, in_sem.at[0])
-    c_to = pltpu.make_async_copy(to_m, to_raw, in_sem.at[1])
-    c_from = pltpu.make_async_copy(from_m, from_raw, in_sem.at[2])
+    TD = T // DC
+    small = [pltpu.make_async_copy(a, b, in_sem.at[2 + i]) for i, (a, b) in enumerate(
+        ((active_h, active), (nbrs_h, nbrs), (rates_h, rates), (lengths_h, lengths)))]
+    c_to = pltpu.make_async_copy(to_m, to_raw, in_sem.at[0])
+    c_from = pltpu.make_async_copy(from_m, from_raw, in_sem.at[1])
+
+    def c_dens(k):
+        return pltpu.make_async_copy(dens.at[pl.ds(k * TD, TD)], dens_v.at[pl.ds(k * TD, TD)], dens_sem.at[k])
+
+    small[0].start()
     c_to.start()
-    c_dens.start()
+    for k in range(DC):
+        c_dens(k).start()
+    for c in small[1:]:
+        c.start()
     c_from.start()
     barrier = pltpu.get_barrier_semaphore()
 
@@ -60,43 +84,37 @@
     def w_copy(c):
         return pltpu.make_async_copy(blocks.at[:, c], wb.at[:, c], w_sem.at[c])
 
-    for h in range(2):
-        act[h * H:(h + 1) * H, :] = spread(active[h:h + 1, :].astype(F32))
-
-    TB = 16
-
-    def group(raw, n):
-        @pl.loop(0, n // TB)
-        def _(i):
-            x = raw[pl.ds(i * TB, TB)].astype(F32)
-            for q in range(C // 8):
-                at = pl.multiple_of(q * n * 8 + i * TB * 8, TB * 8)
-                flat[pl.ds(at, TB * 8), :] = x[:, q * 8:q * 8 + 8].reshape(TB * 8, E)
-
-    def cluster(g, n):
-        return flat[pl.ds(g // 8 * (n * 8) + g % 8, n, stride=8), :]
-
-    def expand(raw, dst):
-        group(raw, M)
-
-        @pl.loop(0, C)
-        def _(g):
-            x = cluster(g, M).astype(BF16)
-            dst[g, 0:M, :] = x
-            dst[g, M:2 * M, :] = x
-
-    c_to.wait()
-    expand(to_raw, to_v)
-    c_dens.wait()
     for lo, hi in ((REACH, C - REACH), (0, REACH), (C - REACH, C)):
         @pl.loop(lo, hi)
         def _(c):
             w_copy(c).start()
 
+    perm[0] = swap16()
+    perm[1] = swap8()
+    small[0].wait()
+    for h in range(2):
+        act[h * H:(h + 1) * H, :] = spread(active[h:h + 1, :].astype(F32))
+
+    def pair(raw, t, c0):
+        x = [raw[pl.ds(t, 16), c0 + i * 16:c0 + i * 16 + 16, :].reshape(256, E) for i in range(2)]
+        return jnp.dot(perm[0], jnp.concatenate(x, axis=1), preferred_element_type=F32)
+
+    def expand(raw, dst):
+        for b in range(M // 16):
+            for c0 in range(0, C, 32):
+                y = pair(raw, b * 16, c0).astype(BF16)
+                for i in range(32):
+                    x = y[i % 16 * 16:i % 16 * 16 + 16, i // 16 * E:(i // 16 + 1) * E]
+                    dst[c0 + i, b * 16:b * 16 + 16, :] = x
+                    dst[c0 + i, M + b * 16:M + b * 16 + 16, :] = x
+
+    c_to.wait()
+    expand(to_raw, to_v)
+    for k in range(DC):
+        c_dens(k).wait()
+
     gid = lax.broadcasted_iota(jnp.int32, (C, E), 0).astype(F32) + first.astype(F32)
     row_out[...] = jnp.where(gid < act[T - 1:T, :], dens_v[T - 1].astype(F32), 0.0)
-    c_from.wait()
-    expand(from_raw, from_v)
     pl.semaphore_wait(barrier, n_space - 1 + n_tm - 1 + corners)
 
     def row_copy(ds):
@@ -133,12 +151,17 @@
             row_copy(ds).start()
     halo_send(0)
 
-    group(dens_v, T)
-
-    @pl.loop(0, C)
-    def _(g):
-        live = (first + g).astype(F32) < act[...]
-        work[REACH + g, 0:T, :] = jnp.where(live, cluster(g, T), 0.0).astype(BF16)
+    @pl.loop(0, T // 128)
+    def _(b):
+        for u in range(8):
+            at = pl.multiple_of(b * 128 + u * 16, 16)
+            live = act[pl.ds(at, 16), :]
+            for c0 in range(0, C, 32):
+                y = pair(dens_v, at, c0)
+                for i in range(32):
+                    x = y[i % 16 * 16:i % 16 * 16 + 16, i // 16 * E:(i // 16 + 1) * E]
+                    x = jnp.where((first + (c0 + i)).astype(F32) < live, x, 0.0)
+                    work[REACH + c0 + i, pl.ds(at, 16), :] = x.astype(BF16)
 
     lane = lax.broadcasted_iota(jnp.int32, (H, 2 * M), 1)
     low = lane < M
@@ -180,17 +203,24 @@
 
     first_row = lax.broadcasted_iota(jnp.int32, (T, E), 0) == 0
 
-    def near_field(c):
-        w_copy(c).wait()
-        rows = [jnp.clip(nbrs[j, c] - first + REACH, 0, C + 2 * REACH - 1) for j in range(J)]
-        picked = jnp.concatenate([work[i] for i in rows], axis=1)
-        w = jnp.concatenate([wb[0, c].reshape(J * E, E), wb[1, c].reshape(J * E, E)], axis=1)
-        both = jnp.dot(picked, w, preferred_element_type=F32)
-        late = both[:, E:]
-        late = jnp.where(first_row, late[T:T + 1, :], pltpu.roll(late[0:T], 1, 0))
-        near[c] = both[0:T, 0:E] + late
-
-    pl.loop(REACH, C - REACH)(near_field)
+    small[1].wait()
+
+    def near_field(c0):
+        for u in range(U):
+            w_copy(c0 + u).wait()
+        for u in range(U):
+            c = c0 + u
+            rows = [jnp.clip(nbrs[j, c] - first + REACH, 0, C + 2 * REACH - 1) for j in range(J)]
+            picked = jnp.concatenate([work[i] for i in rows], axis=1)
+            w = jnp.concatenate([wb[0, c].reshape(J * E, E), wb[1, c].reshape(J * E, E)], axis=1)
+            both = jnp.dot(picked, w, preferred_element_type=F32)
+            late = both[:, E:]
+            late = jnp.where(first_row, late[T:T + 1, :], pltpu.roll(late[0:T], 1, 0))
+            near[c] = both[0:T, 0:E] + late
+
+    @pl.loop(0, (C - 2 * REACH) // U)
+    def _(i):
+        near_field(REACH + i * U)
 
     moment = keep[0]
     for d in range(1, n_space):
@@ -199,6 +229,8 @@
             src_ref=part_out, dst_ref=part_in.at[k], send_sem=part_ssem.at[d], recv_sem=part_rsem.at[k],
             device_id={"tm": tm, "space": k}, device_id_type=MESH).wait_recv()
         moment = moment + part_in[k].astype(F32)
+    small[2].wait()
+    small[3].wait()
     r = rates[...]
     rr = jnp.concatenate([r, r], axis=1)
     span = jnp.where(low, spread(lengths[0:1, :]), spread(lengths[1:2, :]))
@@ -229,6 +261,8 @@
         def _(d=d):
             tot_copy(d).start()
 
+    c_from.wait()
+    expand(from_raw, from_v)
     near_side = jnp.where(lax.rem(sp, 2) == 1, nil, one)
     for k in (near_side, one - near_side):
         other = sp + 2 * k - 1
@@ -241,22 +275,19 @@
                     send_sem=halo_sem.at[0, k, h], recv_sem=halo_sem.at[1, k, h],
                     device_id={"tm": tm, "space": other}, device_id_type=MESH).wait_recv()
 
-            @pl.loop(0, T // 32)
-            def _(i):
-                x = halo[k, pl.ds(i * 32, 32)].astype(F32)
-                flat[pl.ds(pl.multiple_of(i * 32 * REACH, 32 * REACH), 32 * REACH), :] = x.reshape(32 * REACH, E)
-
             begin = k * (REACH + C)
 
-            @pl.loop(0, REACH)
-            def _(g):
-                x = flat[pl.ds(g, T, stride=REACH), :]
-                live = (first - REACH + begin + g).astype(F32) < act[...]
-                work[begin + g, 0:T, :] = jnp.where(live, x, 0.0).astype(BF16)
-
-        @pl.loop(0, REACH)
-        def _(i):
-            near_field(i + k * (C - REACH))
+            for at in range(0, T, 64):
+                x = [halo[k, pl.ds(at + i * 32, 32)].reshape(256, E) for i in range(2)]
+                y = jnp.dot(perm[1], jnp.concatenate(x, axis=1), preferred_element_type=F32)
+                for i in range(2):
+                    live = act[pl.ds(at + i * 32, 32), :]
+                    for g in range(REACH):
+                        x = jnp.where((first - REACH + begin + g).astype(F32) < live,
+                                      y[g * 32:g * 32 + 32, i * E:(i + 1) * E], 0.0)
+                        work[begin + g, pl.ds(at + i * 32, 32), :] = x.astype(BF16)
+
+        near_field(k * (C - REACH))
 
     state[...] = jnp.zeros_like(state)
     for k in range(n_tm - 1):
@@ -330,16 +361,18 @@
         held = pl.pallas_call(
             functools.partial(kernel, n_tm, n_space),
             out_shape=[pltpu.VMEM(s, t) for s, t in kept],
-            in_specs=[anyspec, vspec, pl.BlockSpec(memory_space=pltpu.SMEM), anyspec, anyspec, anyspec, vspec, vspec],
+            in_specs=[anyspec] * 8,
             out_specs=[vspec] * 4,
             scratch_shapes=[
-                vm((T, C, E), BF16), vm((T * C, E), F32), vm((W, T + PAD, E), BF16),
+                vm((T, C, E), BF16), vm((W, T + PAD, E), BF16),
+                vm((2, H), jnp.int32), pltpu.SMEM((J, C), jnp.int32), vm((1, M), F32), vm((2, H), F32),
+                vm((2, 256, 256), BF16),
                 vm((2, T, REACH, E), BF16), vm((8, 128), F32), vm((C, E), F32), vm((W, E), F32),
                 vm((2, C, J, E, E), BF16), vm((M, C, E), BF16), vm((M, C, E), BF16),
                 vm((C, 2 * M, E), BF16),
                 vm((H, 2 * M), BF16), vm((n_space, H, 2 * M), BF16), vm((2, H, 2 * M), F32),
                 vm((16, 2 * M), F32), vm((n_tm, 16, 2 * M), F32), vm((8, 2 * M), F32),
-                dma((3,)), dma((C,)), dma((2, 2, 2)), dma((2, 3)), dma((n_space,)), dma((n_space,)),
+                dma((6,)), dma((DC,)), dma((C,)), dma((2, 2, 2)), dma((2, 3)), dma((n_space,)), dma((n_space,)),
                 dma((n_tm,)), dma((n_tm,)),
             ],
             compiler_params=pltpu.CompilerParams(

time: 23.6 us -> 20.1 us (0.85)
  the two profiles are of different devices: /device:TPU:0 before, /device:TPU:1 now
where the time goes in v1:
time: 20.1 us; the launch traced here: 20 us
  Pallas kernels  20 us (100%)
    pallas_call x1, Pallas kernels, local(): pl.pallas_call(functools.partial(kernel, n_tm, n_space), out_shape=[pltpu...  18 us
    pallas_call x1, Pallas kernels, local(): pl.pallas_call(finish, out_shape=jax.ShapeDtypeStruct((T, C, E), BF16), i...  1.95 us

profile of v1, /device:TPU:1, one launch (start us, length us, event | category | flops | bytes accessed | tf_op | source)
XLA Modules:
  0.0 20.0 jit_solution(11279492319537536653)
XLA Ops:
  0.0 18.0 %shard_map.82 = (f32[32,256,128]{2,1,0:T(8,128)S(1)}, bf16[32,128,128]{2,1,0:T(8,128)(2,1)S(1)}, f32[256,128]{1,0:T(8,128)S(1)}, bf16[256,128]{1,0:T(8,128)(2,1)S(1)}) custom-call(bf16[256,32,128]{2,1,0:T(8,128)(2,1)} %dens.1, s32[2,128]{1,0:T(2,128)} %bitcast.5, s32[8,32]{1,0:T(8,128)} %bitcast.4, bf16[2,32,8,128,128]{4,3,2,1,0:T(8,128)(2,1)} %blocks.1, ...), custom_call_target="tpu_custom_call" | custom-call | tf_op jit(solution)/shard_map/pallas_call | solution.py:361
  18.0 1.9 %shard_map.83 = bf16[256,32,128]{2,1,0:T(8,128)(2,1)} custom-call(f32[32,256,128]{2,1,0:T(8,128)S(1)} %get-tuple-element.9.near, bf16[32,128,128]{2,1,0:T(8,128)(2,1)S(1)} %get-tuple-element.10.from_v, f32[256,128]{1,0:T(8,128)S(1)} %get-tuple-element.11.act, bf16[256,128]{1,0:T(8,128)(2,1)S(1)} %get-tuple-element.12.scaled_o), custom_call_target="tpu_custom_call" | custom-call | tf_op jit(solution)/shard_map/pallas_call | solution.py:382

commit v2 on v1

v2 whole, which is shorter than its diff:
```python
import functools
import math

import jax
import jax.numpy as jnp
from jax import lax
from jax.experimental import pallas as pl
from jax.experimental.pallas import tpu as pltpu
from jax.sharding import PartitionSpec as P

REACH = 8
U = 8
DC = 2
PAD = 16


def PIECES(T):
    return ((0, 4, 0, T // 2), (0, 4, T // 2, T // 2), (4, 2, 0, T), (6, 2, 0, T))


VMEM = 67043328
MESH = pl.DeviceIdType.MESH
F32, BF16 = jnp.float32, jnp.bfloat16


def spread(row):
    return jnp.broadcast_to(row, (128, row.shape[1])).T


def swap16():
    r = lax.broadcasted_iota(jnp.int32, (256, 256), 0)
    s = lax.broadcasted_iota(jnp.int32, (256, 256), 1)
    return jnp.where(s == (r % 16) * 16 + r // 16, 1.0, 0.0).astype(BF16)


def swap8():
    r = lax.broadcasted_iota(jnp.int32, (256, 256), 0)
    s = lax.broadcasted_iota(jnp.int32, (256, 256), 1)
    return jnp.where(s == (r % 8) * 32 + r // 8, 1.0, 0.0).astype(BF16)


def settle(near, from_v, cluster, scaled, act, perm, pot, out, head=None):
    T, E = near(0).shape
    for i in range(0, 8, 2):
        far = jnp.dot(scaled, jnp.concatenate([from_v(i), from_v(i + 1)], axis=1), preferred_element_type=F32)
        for u in range(2):
            live = (cluster + i + u).astype(F32) < act[...]
            x = near(i + u) + far[:, u * E:(u + 1) * E]
            if head is not None:
                head[i + u:i + u + 1, :] = x[0:1, :]
            pot[i + u] = jnp.where(live, x, 0.0).astype(BF16)
    for t in range(0, T, 64):
        x = [pot[:, t + i * 32:t + i * 32 + 32, :].reshape(256, E) for i in range(2)]
        y = jnp.dot(perm[...], jnp.concatenate(x, axis=1), preferred_element_type=F32)
        for i in range(2):
            out[t + i * 32:t + i * 32 + 32] = y[:, i * E:(i + 1) * E].reshape(32, 8, E).astype(BF16)


def kernel(n_tm, n_space, dens, active_h, nbrs_h, blocks, to_m, from_m, rates_h, lengths_h,
           near_far, from_far, act, scaled_o, ready_out, perm_out,
           near, from_v, pot, head, dens_v, work, active, nbrs, rates, lengths, perm,
           halo, row_out, row_pass, row_in, late_out, late_in, wb, to_raw, from_raw, to_v,
           part_out, part_swap, chip_out, part_in, keep, tot_out, tot_swap, tot_chip, tot_in,
           in_sem, dens_sem, w_sem, halo_sem, far_sem, swap_sem, row_sem, late_sem, part_ssem, part_rsem,
           tot_ssem, tot_rsem, ready):
    T, C, E = dens_v.shape
    M = to_raw.shape[0]
    J = wb.shape[2]
    H = T // 2
    tm, sp = lax.axis_index("tm"), lax.axis_index("space")
    first = sp * C
    one, nil = jnp.int32(1), jnp.int32(0)
    odd = lax.rem(sp, 2) == 1
    near_side = jnp.where(odd, nil, one)
    far_side = one - near_side
    chip = sp // 2
    n_chip = n_space // 2
    mate = sp + 2 * near_side - 1
    reach_lo = jnp.where(odd, nil, sp + 2)
    reach_hi = jnp.where(odd, sp - 1, jnp.int32(n_space))

    TD = T // DC
    small = [pltpu.make_async_copy(a, b, in_sem.at[2 + i]) for i, (a, b) in enumerate(
        ((active_h, active), (nbrs_h, nbrs), (rates_h, rates), (lengths_h, lengths)))]
    c_to = pltpu.make_async_copy(to_m, to_raw, in_sem.at[0])
    c_from = pltpu.make_async_copy(from_m, from_raw, in_sem.at[1])

    def c_dens(k):
        return pltpu.make_async_copy(dens.at[pl.ds(k * TD, TD)], dens_v.at[pl.ds(k * TD, TD)], dens_sem.at[k])

    small[0].start()
    for k in range(DC):
        c_dens(k).start()
    c_to.start()
    for c in small[1:]:
        c.start()
    c_from.start()
    barrier = pltpu.get_barrier_semaphore()

    def greet(t, s):
        pl.semaphore_signal(barrier, inc=1, device_id={"tm": t, "space": s}, device_id_type=MESH)

    for d in range(1, n_space):
        greet(tm, lax.rem(sp + d, n_space))

    @pl.loop(tm + 1, n_tm)
    def _(t):
        greet(t, sp)

        @pl.loop(reach_lo, reach_hi)
        def _(s):
            greet(t, s)

    def enter():
        pl.semaphore_wait(barrier, n_space - 1 + tm * n_chip)

        @pl.loop(0, tm)
        def _(t):
            for q in range(n_chip):
                s = jnp.where(chip == q, sp, jnp.where(chip > q, jnp.int32(2 * q), jnp.int32(2 * q + 1)))
                pl.semaphore_signal(ready, inc=1, device_id={"tm": t, "space": s}, device_id_type=MESH)

    def w_copy(c):
        return pltpu.make_async_copy(blocks.at[:, c], wb.at[:, c], w_sem.at[c])

    for lo, n in ((REACH, C - 2 * REACH), (near_side * (C - REACH), REACH), (far_side * (C - REACH), REACH)):
        @pl.loop(0, n)
        def _(i, lo=lo):
            w_copy(lo + i).start()

    perm[...] = swap16()
    perm_out[...] = swap8()
    small[0].wait()
    for h in range(2):
        act[h * H:(h + 1) * H, :] = spread(active[h:h + 1, :].astype(F32))

    def pair(raw, t, c0):
        x = [raw[pl.ds(t, 16), c0 + i * 16:c0 + i * 16 + 16, :].reshape(256, E) for i in range(2)]
        return jnp.dot(perm[...], jnp.concatenate(x, axis=1), preferred_element_type=F32)

    def expand(raw, dst):
        for b in range(M // 16):
            for c0 in range(0, C, 32):
                y = pair(raw, b * 16, c0).astype(BF16)
                for i in range(32):
                    x = y[i % 16 * 16:i % 16 * 16 + 16, i // 16 * E:(i // 16 + 1) * E]
                    dst[c0 + i, b * 16:b * 16 + 16, :] = x
                    dst[c0 + i, M + b * 16:M + b * 16 + 16, :] = x

    def mask(k):
        for t in range(k * TD, (k + 1) * TD, 16):
            live = act[t:t + 16, :]
            for c0 in range(0, C, 32):
                y = pair(dens_v, t, c0)
                for i in range(32):
                    x = y[i % 16 * 16:i % 16 * 16 + 16, i // 16 * E:(i // 16 + 1) * E]
                    x = jnp.where((first + (c0 + i)).astype(F32) < live, x, 0.0)
                    work[REACH + c0 + i, t:t + 16, :] = x.astype(BF16)

    far_there = jnp.where(odd, sp < n_space - 1, sp > 0)

    def near_copy(h):
        return pltpu.make_async_remote_copy(
            src_ref=work.at[pl.ds(REACH + near_side * (C - REACH), REACH), pl.ds(h * H, H), :],
            dst_ref=halo.at[far_side, :, pl.ds(h * H, H), :],
            send_sem=halo_sem.at[0, h], recv_sem=halo_sem.at[1, h],
            device_id={"tm": tm, "space": mate}, device_id_type=MESH)

    def far_copy(p, from_odd=None):
        a, n, lo, size = PIECES(T)[p]
        sender = odd if from_odd is None else from_odd
        src = REACH + jnp.where(odd, jnp.int32(C - a - n), jnp.int32(a))
        dst = jnp.where(sender, jnp.int32(REACH - a - n), jnp.int32(a))
        side = jnp.where(sender, nil, one)
        return pltpu.make_async_remote_copy(
            src_ref=work.at[pl.ds(src, n), pl.ds(lo, size), :],
            dst_ref=halo.at[side, pl.ds(dst, n), pl.ds(lo, size), :],
            send_sem=far_sem.at[0, p], recv_sem=far_sem.at[1, p],
            device_id={"tm": tm, "space": sp + 2 * far_side - 1}, device_id_type=MESH)

    def far_send(ps):
        @pl.when(far_there)
        def _():
            for p in ps:
                far_copy(p).start()

    @pl.when(tm > 0)
    def _():
        enter()

    c_dens(0).wait()
    mask(0)
    for k in range(1, DC):
        c_dens(k).wait()
    @pl.when(tm == 0)
    def _():
        enter()

    far_send((0,))
    near_copy(0).start()

    gid = lax.broadcasted_iota(jnp.int32, (C, E), 0).astype(F32) + first.astype(F32)
    row_out[...] = jnp.where(gid < act[T - 1:T, :], dens_v[T - 1].astype(F32), 0.0)
    for k in range(1, DC):
        mask(k)
    c_to.wait()
    expand(to_raw, to_v)
    far_send((1, 2, 3))
    near_copy(1).start()

    lane = lax.broadcasted_iota(jnp.int32, (H, 2 * M), 1)
    low = lane < M
    GB = 8
    moment = jnp.zeros((H, 2 * M), F32)
    for half in range(2):
        total = jnp.zeros((T, 2 * M), F32)
        for k in range(half * C // GB // 2, (half + 1) * C // GB // 2):
            a = jnp.concatenate([work[REACH + k * GB + i, 0:T, :] for i in range(GB)], axis=1)
            b = jnp.concatenate([to_v[k * GB + i] for i in range(GB)], axis=1)
            total = total + lax.dot_general(a, b, (((1,), (1,)), ((), ())), preferred_element_type=F32)
        moment = moment + jnp.where(low, total[0:H], total[H:T])

    small[2].wait()
    small[3].wait()
    r = rates[...]
    rr = jnp.concatenate([r, r], axis=1)
    span = jnp.where(low, spread(lengths[0:1, :]), spread(lengths[1:2, :]))
    fall = jnp.exp(-rr * span)
    pos = lax.broadcasted_iota(jnp.int32, (H, 2 * M), 0)
    d = 1
    while d < H:
        start = pos < d
        moment = fall * jnp.where(start, 0.0, pltpu.roll(moment, d, 0)) + moment
        fall = fall * jnp.where(start, 1.0, pltpu.roll(fall, d, 0))
        d *= 2
    end_b = jnp.broadcast_to(moment[H - 1:H, :], (8, 2 * M))
    end_a = jnp.broadcast_to(fall[H - 1:H, :], (8, 2 * M))
    low8 = low[0:8]
    roll_b, roll_a = pltpu.roll(end_b, M, 1), pltpu.roll(end_a, M, 1)
    tot_out[0:1] = (end_a * roll_a)[0:1]
    tot_out[1:2] = jnp.where(low8, roll_a * end_b + roll_b, end_a * roll_b + end_b)[0:1]
    moment = jnp.where(pos < 1, 0.0, pltpu.roll(moment, 1, 0))
    fall = jnp.where(pos < 1, 1.0, pltpu.roll(fall, 1, 0))
    moment = moment + fall * jnp.where(low8, 0.0, roll_b)[0:1]
    keep[0] = moment
    keep[1] = fall * jnp.where(low8, 1.0, roll_a)[0:1]
    part_out[...] = moment.astype(BF16)

    row_at = pl.multiple_of(jnp.where(odd, jnp.int32(C - REACH), nil), REACH)
    swaps = [pltpu.make_async_remote_copy(
        src_ref=a, dst_ref=b, send_sem=swap_sem.at[0, i], recv_sem=swap_sem.at[1, i],
        device_id={"tm": tm, "space": mate}, device_id_type=MESH) for i, (a, b) in enumerate(
            ((part_out, part_swap), (tot_out, tot_swap), (row_out.at[pl.ds(row_at, REACH)], row_pass)))]
    for c in swaps:
        c.start()

    first_row = lax.broadcasted_iota(jnp.int32, (T, E), 0) == 0
    small[1].wait()

    def near_field(c0, n, pad, dst, start=0):
        for u in range(n):
            w_copy(c0 + u).wait()
        for u in range(n):
            c = c0 + u
            rows = [jnp.clip(nbrs[j, c] - first + REACH, 0, C + 2 * REACH - 1) for j in range(J)]
            t = T + PAD if pad else T
            picked = jnp.concatenate([work[i, 0:t, :] for i in rows], axis=1)
            w = jnp.concatenate([wb[0, c].reshape(J * E, E), wb[1, c].reshape(J * E, E)], axis=1)
            both = jnp.dot(picked, w, preferred_element_type=F32)
            late = pltpu.roll(both[0:T, E:], 1, 0)
            if pad:
                late = jnp.where(first_row, both[T:T + 1, E:], late)
            else:
                late_out[pl.ds(c, 1), :] = late[0:1, :]
                late = jnp.where(first_row, 0.0, late)
            dst[c - start] = both[0:T, 0:E] + late

    near_field(REACH, U, False, near)

    for c in swaps:
        c.wait_recv()
    both = keep[0] + part_swap[...].astype(F32)
    keep[0] = both
    chip_out[...] = both.astype(BF16)
    tot_chip[0:1] = tot_out[0:1]
    tot_chip[1:2] = tot_out[1:2] + tot_swap[1:2]

    def part_copy(s):
        return pltpu.make_async_remote_copy(
            src_ref=chip_out, dst_ref=part_in.at[chip], send_sem=part_ssem.at[s], recv_sem=part_rsem.at[chip],
            device_id={"tm": tm, "space": s}, device_id_type=MESH)

    @pl.loop(reach_lo, reach_hi)
    def _(s):
        part_copy(s).start()

    def tot_copy(t, s):
        return pltpu.make_async_remote_copy(
            src_ref=tot_chip, dst_ref=tot_in.at[tm, chip], send_sem=tot_ssem.at[t, s], recv_sem=tot_rsem.at[tm, chip],
            device_id={"tm": t, "space": s}, device_id_type=MESH)

    more = tm < n_tm - 1
    less = tm > 0
    own_row = pltpu.make_async_remote_copy(
        src_ref=row_out, dst_ref=row_in.at[pl.ds(REACH, C)], send_sem=row_sem.at[0, 0], recv_sem=row_sem.at[1, 0],
        device_id={"tm": tm + 1, "space": sp}, device_id_type=MESH)
    pass_at = pl.multiple_of(jnp.where(odd, jnp.int32(REACH + C), nil), REACH)
    passes = jnp.logical_and(more, reach_lo < reach_hi)
    pass_row = pltpu.make_async_remote_copy(
        src_ref=row_pass, dst_ref=row_in.at[pl.ds(pass_at, REACH)], send_sem=row_sem.at[0, 1],
        recv_sem=row_sem.at[1, 1], device_id={"tm": tm + 1, "space": sp + 4 * near_side - 2}, device_id_type=MESH)

    def send_later():
        @pl.when(more)
        def _():
            pl.semaphore_wait(ready, (n_tm - 1 - tm) * (1 + reach_hi - reach_lo))

        @pl.when(more)
        def _():
            own_row.start()

        @pl.when(passes)
        def _():
            pass_row.start()

        @pl.loop(tm + 1, n_tm)
        def _(t):
            tot_copy(t, sp).start()

            @pl.loop(reach_lo, reach_hi)
            def _(s):
                tot_copy(t, s).start()

    @pl.when(less)
    def _():
        send_later()

    @pl.loop(1, (C - 2 * REACH) // U)
    def _(i):
        near_field(REACH + i * U, U, False, near)

    for h in range(2):
        near_copy(h).wait_recv()
    for g in range(REACH):
        work[near_side * (REACH + C) + g, 0:T, :] = halo[near_side, g]
    near_field(near_side * (C - REACH), REACH, False, near)

    @pl.when(tm == 0)
    def _():
        send_later()

    c_from.wait()
    expand(from_raw, from_v)

    def far_group(ps, pad):
        a, n = PIECES(T)[ps[0]][:2]

        @pl.when(far_there)
        def _():
            for p in ps:
                far_copy(p, jnp.logical_not(odd)).wait_recv()
            at = jnp.where(odd, jnp.int32(a), jnp.int32(REACH - a - n))
            for g in range(n):
                work[far_side * (REACH + C) + at + g, 0:T, :] = halo[far_side, at + g]

        near_field(jnp.where(odd, jnp.int32(C - REACH + a), jnp.int32(REACH - a - n)), n, pad, near_far,
                   far_side * (C - REACH))

    far_group((0, 1), False)
    late_copy = pltpu.make_async_remote_copy(
        src_ref=late_out, dst_ref=late_in, send_sem=late_sem.at[0], recv_sem=late_sem.at[1],
        device_id={"tm": tm + 1, "space": sp}, device_id_type=MESH)

    @pl.when(more)
    def _():
        late_copy.start()

    @pl.when(tm == 0)
    def _():
        row_in[...] = jnp.zeros_like(row_in)

    @pl.when(less)
    def _():
        own_row.wait_recv()

    @pl.when(jnp.logical_and(less, far_there))
    def _():
        pass_row.wait_recv()

    top = lax.broadcasted_iota(jnp.int32, (PAD, E), 0) == 0

    for i in range(3 * REACH):
        g = far_side * (C - REACH) + i
        r = jnp.broadcast_to(row_in[pl.ds(g, 1), :], (PAD, E))
        work[g, T:T + PAD, :] = jnp.where(top, r, 0.0).astype(BF16)

    far_group((2,), True)
    state = jnp.zeros((1, 2 * M), F32)
    keep[2, 0:1] = state

    @pl.loop(0, tm)
    def _(k):
        for q in range(n_chip):
            pltpu.make_async_remote_copy(
                src_ref=tot_chip, dst_ref=tot_in.at[k, q], send_sem=tot_ssem.at[k, q], recv_sem=tot_rsem.at[k, q],
                device_id={"tm": k, "space": sp}, device_id_type=MESH).wait_recv()
        gain = tot_in[k, 0, 1:2]
        for q in range(1, n_chip):
            gain = gain + tot_in[k, q, 1:2]
        keep[2, 0:1] = tot_in[k, 0, 0:1] * keep[2, 0:1] + gain

    far = keep[0]
    for d in range(1, n_chip):
        k = lax.rem(chip + d, n_chip)
        pltpu.make_async_remote_copy(
            src_ref=chip_out, dst_ref=part_in.at[k], send_sem=part_ssem.at[0], recv_sem=part_rsem.at[k],
            device_id={"tm": tm, "space": mate}, device_id_type=MESH).wait_recv()
        far = far + part_in[k].astype(F32)
    r = rates[...]
    root = jnp.sqrt(2.0 * jnp.concatenate([r, r], axis=1))
    scaled = (keep[1] * keep[2, 0:1] + far) * root
    scaled_o[0:H] = jnp.where(low, scaled, 0.0).astype(BF16)
    scaled_o[H:T] = jnp.where(low, 0.0, scaled).astype(BF16)

    base = near_side * REACH
    scaled = scaled_o[...]
    for b in range(C // 8 - 1):
        settle(lambda i, b=b: near[base + b * 8 + i], lambda i, b=b: from_v[base + b * 8 + i],
               first + base + b * 8, scaled, act, perm_out, pot.at[b], ready_out.at[b], head.at[b])
    for i in range(REACH):
        from_far[i] = from_v[far_side * (C - REACH) + i]

    far_group((3,), True)

    @pl.when(less)
    def _():
        late_copy.wait_recv()

        sub = lax.broadcasted_iota(jnp.int32, (8, E), 0)
        for b in range(C // 8 - 1):
            at = pl.multiple_of(base + b * 8, 8)
            x = head[b] + late_in[pl.ds(at, 8), :]
            live = (sub + (first + at)).astype(F32) < act[0:1, :]
            ready_out[b, 0] = jnp.where(live, x, 0.0).astype(BF16)
        n = PIECES(T)[0][1]
        for u in range(n):
            i = jnp.where(odd, jnp.int32(u), jnp.int32(REACH - n + u))
            near_far[i, 0:1, :] = near_far[i, 0:1, :] + late_in[pl.ds(far_side * (C - REACH) + i, 1), :]

    for c in swaps:
        c.wait_send()

    @pl.loop(reach_lo, reach_hi)
    def _(s):
        part_copy(s).wait_send()

    @pl.loop(tm + 1, n_tm)
    def _(t):
        tot_copy(t, sp).wait_send()

        @pl.loop(reach_lo, reach_hi)
        def _(s):
            tot_copy(t, s).wait_send()

    @pl.when(more)
    def _():
        late_copy.wait_send()

    @pl.when(more)
    def _():
        own_row.wait_send()

    @pl.when(passes)
    def _():
        pass_row.wait_send()

    for h in range(2):
        near_copy(h).wait_send()

    @pl.when(far_there)
    def _():
        for p in range(4):
            far_copy(p).wait_send()


def finish(near, from_v, act, scaled_o, ready, perm, out, pot, out_v, out_sem):
    T = near.shape[1]
    B = ready.shape[0]
    sp = lax.axis_index("space")
    odd = lax.rem(sp, 2) == 1
    one, nil = jnp.int32(1), jnp.int32(0)

    def out_copy(src, block, k, lo, n):
        at = pl.multiple_of(block * 8, 8)
        return pltpu.make_async_copy(src.at[pl.ds(lo, n)], out.at[pl.ds(lo, n), pl.ds(at, 8), :], out_sem.at[k])

    first = jnp.where(odd, nil, one)
    copies = [out_copy(ready.at[b], first + b, b, 0, T) for b in range(B)]
    for c in copies:
        c.start()
    block = jnp.where(odd, jnp.int32(B), nil)
    settle(lambda i: near[i], lambda i: from_v[i], (sp * (B + 1) + block) * 8, scaled_o[...], act, perm, pot, out_v)
    copies.append(out_copy(out_v, block, B, 0, T))
    copies[-1].start()
    for c in copies:
        c.wait()


def solution(mesh):
    n_tm, n_space = mesh.shape["tm"], mesh.shape["space"]

    def local(density, active, neighbours, near_blocks, to_moments, from_moments, decay_rates, lengths):
        T, C, E = density.shape
        J = neighbours.shape[1]
        M = decay_rates.shape[0]
        H, W = T // 2, C + 2 * REACH
        vm = lambda shape, t: pltpu.VMEM(shape, t)
        dma = pltpu.SemaphoreType.DMA
        kept = [((REACH, T, E), F32), ((REACH, 2 * M, E), BF16), ((T, 128), F32), ((T, 2 * M), BF16),
                ((C // 8 - 1, T, 8, E), BF16), ((256, 256), BF16)]
        room = sum(math.prod(s) * jnp.dtype(t).itemsize for s, t in kept) + 32 * 1024
        anyspec = pl.BlockSpec(memory_space=pl.ANY)
        vspec = pl.BlockSpec(memory_space=pltpu.VMEM)
        held = pl.pallas_call(
            functools.partial(kernel, n_tm, n_space),
            out_shape=[pltpu.VMEM(s, t) for s, t in kept],
            in_specs=[anyspec] * 8,
            out_specs=[vspec] * 6,
            scratch_shapes=[
                vm((C, T, E), F32), vm((C, 2 * M, E), BF16), vm((C // 8 - 1, 8, T, E), BF16),
                vm((C // 8 - 1, 8, E), F32),
                vm((T, C, E), BF16), vm((W, T + PAD, E), BF16),
                vm((2, H), jnp.int32), pltpu.SMEM((J, C), jnp.int32), vm((1, M), F32), vm((2, H), F32),
                vm((256, 256), BF16),
                vm((2, REACH, T, E), BF16), vm((C, E), F32), vm((REACH, E), F32), vm((W, E), F32), vm((C, E), F32),
                vm((C, E), F32),
                vm((2, C, J, E, E), BF16), vm((M, C, E), BF16), vm((M, C, E), BF16),
                vm((C, 2 * M, E), BF16),
                vm((H, 2 * M), BF16), vm((H, 2 * M), BF16), vm((H, 2 * M), BF16), vm((n_space // 2, H, 2 * M), BF16),
                vm((3, H, 2 * M), F32), vm((2, 2 * M), F32), vm((2, 2 * M), F32), vm((2, 2 * M), F32),
                vm((n_tm, n_space // 2, 2, 2 * M), F32),
                dma((6,)), dma((DC,)), dma((C,)), dma((2, 2)), dma((2, 4)), dma((2, 3)), dma((2, 2)), dma((2,)),
                dma((n_space,)), dma((n_space // 2,)), dma((n_tm, n_space)), dma((n_tm, n_space // 2)), pltpu.SemaphoreType.REGULAR,
            ],
            compiler_params=pltpu.CompilerParams(
                collective_id=0, has_side_effects=True, vmem_limit_bytes=VMEM - room),
        )(density, active.reshape(2, H), neighbours.T, near_blocks, to_moments, from_moments,
          decay_rates.reshape(1, M), lengths.reshape(2, H))
        return pl.pallas_call(
            finish,
            out_shape=jax.ShapeDtypeStruct((T, C, E), BF16),
            in_specs=[vspec] * 6,
            out_specs=anyspec,
            scratch_shapes=[vm((8, T, E), BF16), vm((T, 8, E), BF16), dma((C // 8,))],
            compiler_params=pltpu.CompilerParams(vmem_limit_bytes=16 * 1024 * 1024),
        )(*held)

    placed = (
        P("tm", "space", None), P("tm"), P("space", None), P(None, "space", None, None, None),
        P(None, "space", None), P(None, "space", None), P(), P("tm"),
    )
    return jax.shard_map(
        local, mesh=mesh, in_specs=placed, out_specs=P("tm", "space", None), check_vma=False)
```

time: 20.1 us -> 16 us (0.80)
  Pallas kernels: 20 us -> 15.9 us
    pallas_call x1, Pallas kernels: 18 us -> 14.2 us  [local(): pl.pallas_call(functools.partial(kernel, n_tm, n_space), out_shape=[pltpu...]
    pallas_call x1, Pallas kernels: 1.95 us -> 1.67 us  [local(): pl.pallas_call(finish, out_shape=jax.ShapeDtypeStruct((T, C, E), BF16), i...]
where the time goes in v2:
time: 16 us; the launch traced here: 15.9 us
  Pallas kernels  15.9 us (99%)
    pallas_call x1, Pallas kernels, local(): pl.pallas_call(functools.partial(kernel, n_tm, n_space), out_shape=[pltpu...  14.2 us
    pallas_call x1, Pallas kernels, local(): pl.pallas_call(finish, out_shape=jax.ShapeDtypeStruct((T, C, E), BF16), i...  1.67 us

profile of v2, /device:TPU:1, one launch (start us, length us, event | category | flops | bytes accessed | tf_op | source)
XLA Modules:
  0.0 15.9 jit_solution(3597623294015236150)
XLA Ops:
  0.0 14.2 %shard_map.82 = (f32[8,256,128]{2,1,0:T(8,128)S(1)}, bf16[8,128,128]{2,1,0:T(8,128)(2,1)S(1)}, f32[256,128]{1,0:T(8,128)S(1)}, bf16[256,128]{1,0:T(8,128)(2,1)S(...) custom-call(bf16[256,32,128]{2,1,0:T(8,128)(2,1)} %dens.1, s32[2,128]{1,0:T(2,128)} %bitcast.5, ...), custom_call_target="tpu_custom_call" | custom-call | tf_op jit(solution)/shard_map/pallas_call | solution.py:524
  14.2 1.7 %shard_map.83 = bf16[256,32,128]{2,1,0:T(8,128)(2,1)} custom-call(f32[8,256,128]{2,1,0:T(8,128)S(1)} %get-tuple-element.11.near, bf16[8,128,128]{2,1,0:T(8,128)(2,1)S(1)} %get-tuple-element.12.from_v, f32[256,128]{1,0:T(8,128)S(1)} %get-tuple-element.13.act, bf16[256,128]{1,0:T(8,128)(2,1)S(1)} %get-tuple-element.14.scaled_o, ...), custom_call_target="tpu_custom_call" | custom-call | tf_op jit(solution)/shard_map/pallas_call | solution.py:549

commit v3 on v2

--- a/solution.py
+++ b/solution.py
@@ -15,7 +15,7 @@
 
 
 def PIECES(T):
-    return ((0, 4, 0, T // 2), (0, 4, T // 2, T // 2), (4, 2, 0, T), (6, 2, 0, T))
+    return ((0, 4, 0, T // 2), (0, 4, T // 2, T // 2), (4, 4, 0, T))
 
 
 VMEM = 67043328
@@ -120,13 +120,23 @@
                 s = jnp.where(chip == q, sp, jnp.where(chip > q, jnp.int32(2 * q), jnp.int32(2 * q + 1)))
                 pl.semaphore_signal(ready, inc=1, device_id={"tm": t, "space": s}, device_id_type=MESH)
 
-    def w_copy(c):
-        return pltpu.make_async_copy(blocks.at[:, c], wb.at[:, c], w_sem.at[c])
-
-    for lo, n in ((REACH, C - 2 * REACH), (near_side * (C - REACH), REACH), (far_side * (C - REACH), REACH)):
+    G = (C - 2 * REACH) // U
+    HALF = REACH // 2
+    near_lo = near_side * (C - REACH)
+    far_lo = (far_side * (C - REACH) + jnp.where(odd, nil, jnp.int32(HALF)),
+              far_side * (C - REACH) + jnp.where(odd, jnp.int32(HALF), nil))
+
+    def w_copy(c, n, k):
+        return pltpu.make_async_copy(blocks.at[:, pl.ds(c, n)], wb.at[:, pl.ds(c, n)], w_sem.at[k])
+
+    @pl.loop(0, C - 2 * REACH)
+    def _(i):
+        w_copy(REACH + i, 1, i // U).start()
+
+    for k, (lo, n) in enumerate(((near_lo, REACH), (far_lo[0], HALF), (far_lo[1], HALF))):
         @pl.loop(0, n)
-        def _(i, lo=lo):
-            w_copy(lo + i).start()
+        def _(i, lo=lo, k=k):
+            w_copy(lo + i, 1, G + k).start()
 
     perm[...] = swap16()
     perm_out[...] = swap8()
@@ -159,15 +169,14 @@
 
     far_there = jnp.where(odd, sp < n_space - 1, sp > 0)
 
-    def near_copy(h):
+    def near_copy(lo, n):
         return pltpu.make_async_remote_copy(
-            src_ref=work.at[pl.ds(REACH + near_side * (C - REACH), REACH), pl.ds(h * H, H), :],
-            dst_ref=halo.at[far_side, :, pl.ds(h * H, H), :],
-            send_sem=halo_sem.at[0, h], recv_sem=halo_sem.at[1, h],
+            src_ref=work.at[pl.ds(REACH + near_side * (C - REACH), REACH), pl.ds(lo, n), :],
+            dst_ref=halo.at[far_side, :, pl.ds(lo, n), :],
+            send_sem=halo_sem.at[0], recv_sem=halo_sem.at[1],
             device_id={"tm": tm, "space": mate}, device_id_type=MESH)
 
-    def far_copy(p, from_odd=None):
-        a, n, lo, size = PIECES(T)[p]
+    def far_copy(a, n, lo, size, k, from_odd=None):
         sender = odd if from_odd is None else from_odd
         src = REACH + jnp.where(odd, jnp.int32(C - a - n), jnp.int32(a))
         dst = jnp.where(sender, jnp.int32(REACH - a - n), jnp.int32(a))
@@ -175,14 +184,14 @@
         return pltpu.make_async_remote_copy(
             src_ref=work.at[pl.ds(src, n), pl.ds(lo, size), :],
             dst_ref=halo.at[side, pl.ds(dst, n), pl.ds(lo, size), :],
-            send_sem=far_sem.at[0, p], recv_sem=far_sem.at[1, p],
+            send_sem=far_sem.at[0], recv_sem=far_sem.at[1 + k],
             device_id={"tm": tm, "space": sp + 2 * far_side - 1}, device_id_type=MESH)
 
     def far_send(ps):
         @pl.when(far_there)
         def _():
             for p in ps:
-                far_copy(p).start()
+                far_copy(*PIECES(T)[p], PIECES(T)[p][0] // HALF).start()
 
     @pl.when(tm > 0)
     def _():
@@ -197,7 +206,7 @@
         enter()
 
     far_send((0,))
-    near_copy(0).start()
+    near_copy(0, H).start()
 
     gid = lax.broadcasted_iota(jnp.int32, (C, E), 0).astype(F32) + first.astype(F32)
     row_out[...] = jnp.where(gid < act[T - 1:T, :], dens_v[T - 1].astype(F32), 0.0)
@@ -205,8 +214,8 @@
         mask(k)
     c_to.wait()
     expand(to_raw, to_v)
-    far_send((1, 2, 3))
-    near_copy(1).start()
+    far_send((1, 2))
+    near_copy(H, H).start()
 
     lane = lax.broadcasted_iota(jnp.int32, (H, 2 * M), 1)
     low = lane < M
@@ -257,9 +266,8 @@
     first_row = lax.broadcasted_iota(jnp.int32, (T, E), 0) == 0
     small[1].wait()
 
-    def near_field(c0, n, pad, dst, start=0):
-        for u in range(n):
-            w_copy(c0 + u).wait()
+    def near_field(c0, n, pad, dst, k, start=0):
+        w_copy(c0, n, k).wait()
         for u in range(n):
             c = c0 + u
             rows = [jnp.clip(nbrs[j, c] - first + REACH, 0, C + 2 * REACH - 1) for j in range(J)]
@@ -275,7 +283,7 @@
                 late = jnp.where(first_row, 0.0, late)
             dst[c - start] = both[0:T, 0:E] + late
 
-    near_field(REACH, U, False, near)
+    near_field(REACH, U, False, near, 0)
 
     for c in swaps:
         c.wait_recv()
@@ -296,7 +304,7 @@
 
     def tot_copy(t, s):
         return pltpu.make_async_remote_copy(
-            src_ref=tot_chip, dst_ref=tot_in.at[tm, chip], send_sem=tot_ssem.at[t, s], recv_sem=tot_rsem.at[tm, chip],
+            src_ref=tot_chip, dst_ref=tot_in.at[tm, chip], send_sem=tot_ssem.at[t], recv_sem=tot_rsem.at[tm],
             device_id={"tm": t, "space": s}, device_id_type=MESH)
 
     more = tm < n_tm - 1
@@ -337,13 +345,12 @@
 
     @pl.loop(1, (C - 2 * REACH) // U)
     def _(i):
-        near_field(REACH + i * U, U, False, near)
-
-    for h in range(2):
-        near_copy(h).wait_recv()
+        near_field(REACH + i * U, U, False, near, i)
+
+    near_copy(0, T).wait_recv()
     for g in range(REACH):
         work[near_side * (REACH + C) + g, 0:T, :] = halo[near_side, g]
-    near_field(near_side * (C - REACH), REACH, False, near)
+    near_field(near_lo, REACH, False, near, G)
 
     @pl.when(tm == 0)
     def _():
@@ -352,21 +359,19 @@
     c_from.wait()
     expand(from_raw, from_v)
 
-    def far_group(ps, pad):
-        a, n = PIECES(T)[ps[0]][:2]
+    def far_group(k, pad):
+        a = k * HALF
 
         @pl.when(far_there)
         def _():
-            for p in ps:
-                far_copy(p, jnp.logical_not(odd)).wait_recv()
-            at = jnp.where(odd, jnp.int32(a), jnp.int32(REACH - a - n))
-            for g in range(n):
+            far_copy(a, HALF, 0, T, k, jnp.logical_not(odd)).wait_recv()
+            at = jnp.where(odd, jnp.int32(a), jnp.int32(REACH - a - HALF))
+            for g in range(HALF):
                 work[far_side * (REACH + C) + at + g, 0:T, :] = halo[far_side, at + g]
 
-        near_field(jnp.where(odd, jnp.int32(C - REACH + a), jnp.int32(REACH - a - n)), n, pad, near_far,
-                   far_side * (C - REACH))
-
-    far_group((0, 1), False)
+        near_field(far_lo[k], HALF, pad, near_far, G + 1 + k, far_side * (C - REACH))
+
+    far_group(0, False)
     late_copy = pltpu.make_async_remote_copy(
         src_ref=late_out, dst_ref=late_in, send_sem=late_sem.at[0], recv_sem=late_sem.at[1],
         device_id={"tm": tm + 1, "space": sp}, device_id_type=MESH)
@@ -394,16 +399,14 @@
         r = jnp.broadcast_to(row_in[pl.ds(g, 1), :], (PAD, E))
         work[g, T:T + PAD, :] = jnp.where(top, r, 0.0).astype(BF16)
 
-    far_group((2,), True)
     state = jnp.zeros((1, 2 * M), F32)
     keep[2, 0:1] = state
 
     @pl.loop(0, tm)
     def _(k):
-        for q in range(n_chip):
-            pltpu.make_async_remote_copy(
-                src_ref=tot_chip, dst_ref=tot_in.at[k, q], send_sem=tot_ssem.at[k, q], recv_sem=tot_rsem.at[k, q],
-                device_id={"tm": k, "space": sp}, device_id_type=MESH).wait_recv()
+        pltpu.make_async_remote_copy(
+            src_ref=tot_in.at[k], dst_ref=tot_in.at[k], send_sem=tot_ssem.at[k], recv_sem=tot_rsem.at[k],
+            device_id={"tm": k, "space": sp}, device_id_type=MESH).wait_recv()
         gain = tot_in[k, 0, 1:2]
         for q in range(1, n_chip):
             gain = gain + tot_in[k, q, 1:2]
@@ -430,7 +433,7 @@
     for i in range(REACH):
         from_far[i] = from_v[far_side * (C - REACH) + i]
 
-    far_group((3,), True)
+    far_group(1, True)
 
     @pl.when(less)
     def _():
@@ -442,7 +445,7 @@
             x = head[b] + late_in[pl.ds(at, 8), :]
             live = (sub + (first + at)).astype(F32) < act[0:1, :]
             ready_out[b, 0] = jnp.where(live, x, 0.0).astype(BF16)
-        n = PIECES(T)[0][1]
+        n = HALF
         for u in range(n):
             i = jnp.where(odd, jnp.int32(u), jnp.int32(REACH - n + u))
             near_far[i, 0:1, :] = near_far[i, 0:1, :] + late_in[pl.ds(far_side * (C - REACH) + i, 1), :]
@@ -454,13 +457,15 @@
     def _(s):
         part_copy(s).wait_send()
 
-    @pl.loop(tm + 1, n_tm)
-    def _(t):
-        tot_copy(t, sp).wait_send()
-
-        @pl.loop(reach_lo, reach_hi)
-        def _(s):
-            tot_copy(t, s).wait_send()
+    for j in range(n_chip):
+        @pl.when(reach_hi - reach_lo == 2 * j)
+        def _(j=j):
+            @pl.loop(tm + 1, n_tm)
+            def _(t):
+                sent = tot_in.at[pl.ds(0, 1 + 2 * j), 0]
+                pltpu.make_async_remote_copy(
+                    src_ref=sent, dst_ref=sent, send_sem=tot_ssem.at[t], recv_sem=tot_rsem.at[t],
+                    device_id={"tm": t, "space": sp}, device_id_type=MESH).wait_send()
 
     @pl.when(more)
     def _():
@@ -474,13 +479,11 @@
     def _():
         pass_row.wait_send()
 
-    for h in range(2):
-        near_copy(h).wait_send()
+    near_copy(0, T).wait_send()
 
     @pl.when(far_there)
     def _():
-        for p in range(4):
-            far_copy(p).wait_send()
+        far_copy(0, REACH, 0, T, 0).wait_send()
 
 
 def finish(near, from_v, act, scaled_o, ready, perm, out, pot, out_v, out_sem):
@@ -539,8 +542,8 @@
                 vm((H, 2 * M), BF16), vm((H, 2 * M), BF16), vm((H, 2 * M), BF16), vm((n_space // 2, H, 2 * M), BF16),
                 vm((3, H, 2 * M), F32), vm((2, 2 * M), F32), vm((2, 2 * M), F32), vm((2, 2 * M), F32),
                 vm((n_tm, n_space // 2, 2, 2 * M), F32),
-                dma((6,)), dma((DC,)), dma((C,)), dma((2, 2)), dma((2, 4)), dma((2, 3)), dma((2, 2)), dma((2,)),
-                dma((n_space,)), dma((n_space // 2,)), dma((n_tm, n_space)), dma((n_tm, n_space // 2)), pltpu.SemaphoreType.REGULAR,
+                dma((6,)), dma((DC,)), dma(((C - 2 * REACH) // U + 3,)), dma((2,)), dma((3,)), dma((2, 3)), dma((2, 2)), dma((2,)),
+                dma((n_space,)), dma((n_space // 2,)), dma((n_tm,)), dma((n_tm,)), pltpu.SemaphoreType.REGULAR,
             ],
             compiler_params=pltpu.CompilerParams(
                 collective_id=0, has_side_effects=True, vmem_limit_bytes=VMEM - room),

time: 16 us -> 15.3 us (0.956)
  Pallas kernels: 15.9 us -> 15.1 us
    pallas_call x1, Pallas kernels: 14.2 us -> 13.4 us  [local(): pl.pallas_call(functools.partial(kernel, n_tm, n_space), out_shape=[pltpu...]
where the time goes in v3:
time: 15.3 us; the launch traced here: 15.1 us
  Pallas kernels  15.1 us (99%)
    pallas_call x1, Pallas kernels, local(): pl.pallas_call(functools.partial(kernel, n_tm, n_space), out_shape=[pltpu...  13.4 us
    pallas_call x1, Pallas kernels, local(): pl.pallas_call(finish, out_shape=jax.ShapeDtypeStruct((T, C, E), BF16), i...  1.66 us

profile of v3, /device:TPU:1, one launch (start us, length us, event | category | flops | bytes accessed | tf_op | source)
XLA Modules:
  0.0 15.1 jit_solution(10678949558311306941)
XLA Ops:
  0.0 13.4 %shard_map.82 = (f32[8,256,128]{2,1,0:T(8,128)S(1)}, bf16[8,128,128]{2,1,0:T(8,128)(2,1)S(1)}, f32[256,128]{1,0:T(8,128)S(1)}, bf16[256,128]{1,0:T(8,128)(2,1)S(...) custom-call(bf16[256,32,128]{2,1,0:T(8,128)(2,1)} %dens.1, s32[2,128]{1,0:T(2,128)} %bitcast.5, ...), custom_call_target="tpu_custom_call" | custom-call | tf_op jit(solution)/shard_map/pallas_call | solution.py:527
  13.5 1.7 %shard_map.83 = bf16[256,32,128]{2,1,0:T(8,128)(2,1)} custom-call(f32[8,256,128]{2,1,0:T(8,128)S(1)} %get-tuple-element.11.near, bf16[8,128,128]{2,1,0:T(8,128)(2,1)S(1)} %get-tuple-element.12.from_v, f32[256,128]{1,0:T(8,128)S(1)} %get-tuple-element.13.act, bf16[256,128]{1,0:T(8,128)(2,1)S(1)} %get-tuple-element.14.scaled_o, ...), custom_call_target="tpu_custom_call" | custom-call | tf_op jit(solution)/shard_map/pallas_call | solution.py:552

commit v4 on v3

--- a/solution.py
+++ b/solution.py
@@ -11,6 +11,7 @@
 REACH = 8
 U = 8
 DC = 2
+SPLIT = 4
 PAD = 16
 
 
@@ -39,7 +40,7 @@
     return jnp.where(s == (r % 8) * 32 + r // 8, 1.0, 0.0).astype(BF16)
 
 
-def settle(near, from_v, cluster, scaled, act, perm, pot, out, head=None):
+def settle(near, from_v, cluster, scaled, act, perm, pot, out, head=None, sent=None):
     T, E = near(0).shape
     for i in range(0, 8, 2):
         far = jnp.dot(scaled, jnp.concatenate([from_v(i), from_v(i + 1)], axis=1), preferred_element_type=F32)
@@ -54,6 +55,8 @@
         y = jnp.dot(perm[...], jnp.concatenate(x, axis=1), preferred_element_type=F32)
         for i in range(2):
             out[t + i * 32:t + i * 32 + 32] = y[:, i * E:(i + 1) * E].reshape(32, 8, E).astype(BF16)
+        if sent is not None:
+            sent(t, 64)
 
 
 def kernel(n_tm, n_space, dens, active_h, nbrs_h, blocks, to_m, from_m, rates_h, lengths_h,
@@ -61,7 +64,7 @@
            near, from_v, pot, head, dens_v, work, active, nbrs, rates, lengths, perm,
            halo, row_out, row_pass, row_in, late_out, late_in, wb, to_raw, from_raw, to_v,
            part_out, part_swap, chip_out, part_in, keep, tot_out, tot_swap, tot_chip, tot_in,
-           in_sem, dens_sem, w_sem, halo_sem, far_sem, swap_sem, row_sem, late_sem, part_ssem, part_rsem,
+           in_sem, dens_sem, w_sem, halo_sem, far_sem, swap_sem, row_sem, late_sem, part_sem,
            tot_ssem, tot_rsem, ready):
     T, C, E = dens_v.shape
     M = to_raw.shape[0]
@@ -295,7 +298,7 @@
 
     def part_copy(s):
         return pltpu.make_async_remote_copy(
-            src_ref=chip_out, dst_ref=part_in.at[chip], send_sem=part_ssem.at[s], recv_sem=part_rsem.at[chip],
+            src_ref=chip_out, dst_ref=part_in.at[chip], send_sem=part_sem.at[0], recv_sem=part_sem.at[1],
             device_id={"tm": tm, "space": s}, device_id_type=MESH)
 
     @pl.loop(reach_lo, reach_hi)
@@ -304,7 +307,7 @@
 
     def tot_copy(t, s):
         return pltpu.make_async_remote_copy(
-            src_ref=tot_chip, dst_ref=tot_in.at[tm, chip], send_sem=tot_ssem.at[t], recv_sem=tot_rsem.at[tm],
+            src_ref=tot_chip, dst_ref=tot_in.at[tm, chip], send_sem=tot_ssem.at[t], recv_sem=tot_rsem.at[0],
             device_id={"tm": t, "space": s}, device_id_type=MESH)
 
     more = tm < n_tm - 1
@@ -402,23 +405,29 @@
     state = jnp.zeros((1, 2 * M), F32)
     keep[2, 0:1] = state
 
+    for j in range(1, n_tm):
+        @pl.when(tm == j)
+        def _(j=j):
+            came = tot_in.at[pl.ds(0, j)]
+            pltpu.make_async_remote_copy(
+                src_ref=came, dst_ref=came, send_sem=tot_ssem.at[0], recv_sem=tot_rsem.at[0],
+                device_id={"tm": tm - 1, "space": sp}, device_id_type=MESH).wait_recv()
+
     @pl.loop(0, tm)
     def _(k):
-        pltpu.make_async_remote_copy(
-            src_ref=tot_in.at[k], dst_ref=tot_in.at[k], send_sem=tot_ssem.at[k], recv_sem=tot_rsem.at[k],
-            device_id={"tm": k, "space": sp}, device_id_type=MESH).wait_recv()
         gain = tot_in[k, 0, 1:2]
         for q in range(1, n_chip):
             gain = gain + tot_in[k, q, 1:2]
         keep[2, 0:1] = tot_in[k, 0, 0:1] * keep[2, 0:1] + gain
 
     far = keep[0]
+    if n_chip > 1:
+        came = part_in.at[pl.ds(0, n_chip - 1)]
+        pltpu.make_async_remote_copy(
+            src_ref=came, dst_ref=came, send_sem=part_sem.at[0], recv_sem=part_sem.at[1],
+            device_id={"tm": tm, "space": mate}, device_id_type=MESH).wait_recv()
     for d in range(1, n_chip):
-        k = lax.rem(chip + d, n_chip)
-        pltpu.make_async_remote_copy(
-            src_ref=chip_out, dst_ref=part_in.at[k], send_sem=part_ssem.at[0], recv_sem=part_rsem.at[k],
-            device_id={"tm": tm, "space": mate}, device_id_type=MESH).wait_recv()
-        far = far + part_in[k].astype(F32)
+        far = far + part_in[lax.rem(chip + d, n_chip)].astype(F32)
     r = rates[...]
     root = jnp.sqrt(2.0 * jnp.concatenate([r, r], axis=1))
     scaled = (keep[1] * keep[2, 0:1] + far) * root
@@ -453,18 +462,20 @@
     for c in swaps:
         c.wait_send()
 
-    @pl.loop(reach_lo, reach_hi)
-    def _(s):
-        part_copy(s).wait_send()
-
     for j in range(n_chip):
         @pl.when(reach_hi - reach_lo == 2 * j)
         def _(j=j):
+            if j > 0:
+                sent = halo.at[0, pl.ds(0, j)]
+                pltpu.make_async_remote_copy(
+                    src_ref=sent, dst_ref=sent, send_sem=part_sem.at[0], recv_sem=part_sem.at[1],
+                    device_id={"tm": tm, "space": mate}, device_id_type=MESH).wait_send()
+
             @pl.loop(tm + 1, n_tm)
             def _(t):
                 sent = tot_in.at[pl.ds(0, 1 + 2 * j), 0]
                 pltpu.make_async_remote_copy(
-                    src_ref=sent, dst_ref=sent, send_sem=tot_ssem.at[t], recv_sem=tot_rsem.at[t],
+                    src_ref=sent, dst_ref=sent, send_sem=tot_ssem.at[t], recv_sem=tot_rsem.at[0],
                     device_id={"tm": t, "space": sp}, device_id_type=MESH).wait_send()
 
     @pl.when(more)
@@ -498,15 +509,15 @@
         return pltpu.make_async_copy(src.at[pl.ds(lo, n)], out.at[pl.ds(lo, n), pl.ds(at, 8), :], out_sem.at[k])
 
     first = jnp.where(odd, nil, one)
-    copies = [out_copy(ready.at[b], first + b, b, 0, T) for b in range(B)]
-    for c in copies:
-        c.start()
+    for b in range(B):
+        for lo in range(0, T, T // SPLIT):
+            out_copy(ready.at[b], first + b, b, lo, T // SPLIT).start()
     block = jnp.where(odd, jnp.int32(B), nil)
-    settle(lambda i: near[i], lambda i: from_v[i], (sp * (B + 1) + block) * 8, scaled_o[...], act, perm, pot, out_v)
-    copies.append(out_copy(out_v, block, B, 0, T))
-    copies[-1].start()
-    for c in copies:
-        c.wait()
+    settle(lambda i: near[i], lambda i: from_v[i], (sp * (B + 1) + block) * 8, scaled_o[...], act, perm, pot, out_v,
+           sent=lambda lo, n: out_copy(out_v, block, B, lo, n).start())
+    for b in range(B):
+        out_copy(ready.at[b], first + b, b, 0, T).wait()
+    out_copy(out_v, block, B, 0, T).wait()
 
 
 def solution(mesh):
@@ -543,7 +554,7 @@
                 vm((3, H, 2 * M), F32), vm((2, 2 * M), F32), vm((2, 2 * M), F32), vm((2, 2 * M), F32),
                 vm((n_tm, n_space // 2, 2, 2 * M), F32),
                 dma((6,)), dma((DC,)), dma(((C - 2 * REACH) // U + 3,)), dma((2,)), dma((3,)), dma((2, 3)), dma((2, 2)), dma((2,)),
-                dma((n_space,)), dma((n_space // 2,)), dma((n_tm,)), dma((n_tm,)), pltpu.SemaphoreType.REGULAR,
+                dma((2,)), dma((n_tm,)), dma((1,)), pltpu.SemaphoreType.REGULAR,
             ],
             compiler_params=pltpu.CompilerParams(
                 collective_id=0, has_side_effects=True, vmem_limit_bytes=VMEM - room),

time: 15.3 us -> 15.1 us (0.987)
  Pallas kernels: 15.1 us -> 14.9 us
where the time goes in v4:
time: 15.1 us; the launch traced here: 15 us
  Pallas kernels  14.9 us (99%)
    pallas_call x1, Pallas kernels, local(): pl.pallas_call(functools.partial(kernel, n_tm, n_space), out_shape=[pltpu...  13.4 us
    pallas_call x1, Pallas kernels, local(): pl.pallas_call(finish, out_shape=jax.ShapeDtypeStruct((T, C, E), BF16), i...  1.6 us

profile of v4, /device:TPU:1, one launch (start us, length us, event | category | flops | bytes accessed | tf_op | source)
XLA Modules:
  0.0 15.0 jit_solution(342940934246134801)
XLA Ops:
  0.0 13.4 %shard_map.82 = (f32[8,256,128]{2,1,0:T(8,128)S(1)}, bf16[8,128,128]{2,1,0:T(8,128)(2,1)S(1)}, f32[256,128]{1,0:T(8,128)S(1)}, bf16[256,128]{1,0:T(8,128)(2,1)S(...) custom-call(bf16[256,32,128]{2,1,0:T(8,128)(2,1)} %dens.1, s32[2,128]{1,0:T(2,128)} %bitcast.5, ...), custom_call_target="tpu_custom_call" | custom-call | tf_op jit(solution)/shard_map/pallas_call | solution.py:538
  13.4 1.6 %shard_map.83 = bf16[256,32,128]{2,1,0:T(8,128)(2,1)} custom-call(f32[8,256,128]{2,1,0:T(8,128)S(1)} %get-tuple-element.11.near, bf16[8,128,128]{2,1,0:T(8,128)(2,1)S(1)} %get-tuple-element.12.from_v, f32[256,128]{1,0:T(8,128)S(1)} %get-tuple-element.13.act, bf16[256,128]{1,0:T(8,128)(2,1)S(1)} %get-tuple-element.14.scaled_o, ...), custom_call_target="tpu_custom_call" | custom-call | tf_op jit(solution)/shard_map/pallas_call | solution.py:563

commit v5 on v4

--- a/solution.py
+++ b/solution.py
@@ -208,8 +208,8 @@
     def _():
         enter()
 
+    near_copy(0, H).start()
     far_send((0,))
-    near_copy(0, H).start()
 
     gid = lax.broadcasted_iota(jnp.int32, (C, E), 0).astype(F32) + first.astype(F32)
     row_out[...] = jnp.where(gid < act[T - 1:T, :], dens_v[T - 1].astype(F32), 0.0)
@@ -217,8 +217,8 @@
         mask(k)
     c_to.wait()
     expand(to_raw, to_v)
+    near_copy(H, H).start()
     far_send((1, 2))
-    near_copy(H, H).start()
 
     lane = lax.broadcasted_iota(jnp.int32, (H, 2 * M), 1)
     low = lane < M

time: 15.1 us -> 15.1 us (level)
  no operation moved by 1% of the time
where the time goes in v5:
time: 15.1 us; the launch traced here: 15 us
  Pallas kernels  14.9 us (99%)
    pallas_call x1, Pallas kernels, local(): pl.pallas_call(functools.partial(kernel, n_tm, n_space), out_shape=[pltpu...  13.4 us
    pallas_call x1, Pallas kernels, local(): pl.pallas_call(finish, out_shape=jax.ShapeDtypeStruct((T, C, E), BF16), i...  1.6 us

profile of v5, /device:TPU:1, one launch (start us, length us, event | category | flops | bytes accessed | tf_op | source)
XLA Modules:
  0.0 15.0 jit_solution(3735066936996282393)
XLA Ops:
  0.0 13.4 %shard_map.82 = (f32[8,256,128]{2,1,0:T(8,128)S(1)}, bf16[8,128,128]{2,1,0:T(8,128)(2,1)S(1)}, f32[256,128]{1,0:T(8,128)S(1)}, bf16[256,128]{1,0:T(8,128)(2,1)S(...) custom-call(bf16[256,32,128]{2,1,0:T(8,128)(2,1)} %dens.1, s32[2,128]{1,0:T(2,128)} %bitcast.5, ...), custom_call_target="tpu_custom_call" | custom-call | tf_op jit(solution)/shard_map/pallas_call | solution.py:538
  13.4 1.6 %shard_map.83 = bf16[256,32,128]{2,1,0:T(8,128)(2,1)} custom-call(f32[8,256,128]{2,1,0:T(8,128)S(1)} %get-tuple-element.11.near, bf16[8,128,128]{2,1,0:T(8,128)(2,1)S(1)} %get-tuple-element.12.from_v, f32[256,128]{1,0:T(8,128)S(1)} %get-tuple-element.13.act, bf16[256,128]{1,0:T(8,128)(2,1)S(1)} %get-tuple-element.14.scaled_o, ...), custom_call_target="tpu_custom_call" | custom-call | tf_op jit(solution)/shard_map/pallas_call | solution.py:563
